TPU v7x, 32 devices: a whole 2x2x4 slice. The times are simulated.
32 devices in a mesh: up: 8 (over y, x, core), dn: 4 (over z).
Axes of the slice: x: 2, y: 2, z: 4, core: 2. Of those that a mesh axis runs over, the one named last changes fastest.
Arguments:
- start_vector: bfloat16 [13312, 13312], P('up', 'dn'), may hold values from -6 to 6
- hop_tiles: bfloat16 [104, 5, 128, 128], replicated, may hold values from -0.5 to 0.5
- tile_columns: int32 [104, 5], replicated, may hold values from 0 to 103, as said below
- tile_signs: int32 [104, 5], replicated, may hold values from 0 to 1
- occupation: int32 [16, 13312], replicated, may hold values from 0 to 1, as said below
Outputs:
- next_vector: bfloat16 [13312, 13312], P('up', 'dn')
- alphas: float32 [2], replicated
- betas: float32 [2], replicated
Inputs may be any that keep to these rules, and one draw needn't show every extreme that they name: Each row of tile_columns names 5 different tile columns. Every column of occupation holds exactly 8 ones.
All inputs are finite; a program needn't handle non-finite values.
Results may differ from a plain program's by a relative error of at most 0.0065.
Values may be sent and summed in bfloat16 or wider, within the bound.
A program may use at most 256 MiB of HBM per device.

v0:
```python
import jax
import jax.numpy as jnp
from jax import lax
from jax.sharding import PartitionSpec as P

STEPS = 2
coupling = 4.0


def hop_lead(matrix, signed, tile_columns):
    layout = matrix.shape
    tile_width = signed.shape[-1]
    cube = matrix.reshape(layout[0] // tile_width, tile_width, -1)
    picked = cube[tile_columns]
    result = jnp.einsum("ikab,ikbm->iam", signed, picked, preferred_element_type=jnp.float32)
    return result.reshape(layout).astype(jnp.bfloat16)


def body(start_vector, hop_tiles, tile_columns, tile_signs, occupation):
    signed = hop_tiles * (1 - 2 * tile_signs).astype(jnp.bfloat16)[:, :, None, None]
    rows_local, cols_local = start_vector.shape
    count_up = lax.axis_size("up")
    count_down = lax.axis_size("dn")
    row_start = lax.axis_index("up") * rows_local
    col_start = lax.axis_index("dn") * cols_local
    block_rows, block_cols = start_vector.shape
    occ_rows = lax.dynamic_slice_in_dim(occupation, row_start, block_rows, 1).astype(jnp.bfloat16)
    occ_cols = lax.dynamic_slice_in_dim(occupation, col_start, block_cols, 1).astype(jnp.bfloat16)
    diagonal = coupling * jnp.einsum(
        "sa,sb->ab", occ_rows, occ_cols, preferred_element_type=jnp.float32
    )
    vector = start_vector.astype(jnp.float32)
    total = lax.psum(jnp.sum(vector * vector), ("up", "dn"))
    vector = vector / jnp.maximum(jnp.sqrt(total), 1.0)
    length = total / jnp.maximum(total, 1.0)
    previous = jnp.zeros_like(vector)
    beta_value = jnp.float32(0.0)
    alpha_list = []
    beta_list = []
    for iteration in range(STEPS):
        rounded = vector.astype(jnp.bfloat16)
        cube = rounded.reshape(block_rows, count_up, block_cols // count_up)
        up_part = lax.all_to_all(cube, "up", split_axis=1, concat_axis=0, tiled=True)
        up_whole = up_part.reshape(up_part.shape[0], up_part.shape[2])
        up_hopped = hop_lead(up_whole, signed, tile_columns).reshape(up_part.shape)
        moved = lax.all_to_all(up_hopped, "up", split_axis=0, concat_axis=1, tiled=True)
        hopped_up = moved.reshape(block_rows, block_cols)
        flipped = rounded.T.reshape(block_cols, count_down, block_rows // count_down)
        part = lax.all_to_all(flipped, "dn", split_axis=1, concat_axis=0, tiled=True)
        whole = part.reshape(part.shape[0], part.shape[2])
        hopped = hop_lead(whole, signed, tile_columns).reshape(part.shape)
        returned = lax.all_to_all(hopped, "dn", split_axis=0, concat_axis=1, tiled=True)
        hopped_down = returned.reshape(block_cols, block_rows).T
        work = (
            hopped_up.astype(jnp.float32)
            + hopped_down.astype(jnp.float32)
            + diagonal * vector
            - beta_value * previous
        )
        intersect, square = lax.psum((jnp.sum(work * vector), jnp.sum(work * work)), ("up", "dn"))
        work = work - intersect * vector
        residual = square - 2.0 * intersect * intersect + intersect * intersect * length
        beta_value = jnp.sqrt(jnp.maximum(residual, 1.0))
        length = residual / jnp.maximum(residual, 1.0)
        previous = vector
        vector = work / beta_value
        alpha_list.append(intersect)
        beta_list.append(beta_value)
    final = vector.astype(jnp.bfloat16)
    return (final, jnp.stack(alpha_list), jnp.stack(beta_list))


def solution(mesh):
    placed = (P("up", "dn"), P(), P(), P(), P())
    return jax.shard_map(
        body, mesh=mesh, in_specs=placed, out_specs=(P("up", "dn"), P(), P()), check_vma=False
    )
```

profile of v0, /device:TPU:12, one launch (start us, length us, event | category | flops | bytes accessed | tf_op | source)
XLA Modules:
  0.0 2605.0 jit_solution(15196336587195113989)
XLA Ops:
  11.1 41.6 %psum.35 = f32[]{:T(128)} all-reduce(f32[]{:T(128)} %fusion), channel_id=1, replica_groups=mesh['up'=8,'dn'=4] {'up','dn'}, use_global_device_ids=true, to_apply=%region_1.0 | all-reduce | flops 1 | bytes 8 | tf_op jit(solution)/shard_map/psum | solution.py:33
  80.3 127.1 %all_to_all.96 = bf16[1664,8,416]{0,2,1:T(8,128)(2,1)} all-to-all(bf16[1664,8,416]{0,2,1:T(8,128)(2,1)} %bitcast.112), channel_id=1, replica_groups=mesh['up'=8,'dn'=4] {'up'}, dimensions={1} | all-to-all | bytes 22151168 | tf_op jit(solution)/shard_map/all_to_all | solution.py:43
  337.4 77.7 %reshape.155 = bf16[13312,1,416]{2,1,0:T(2,128)(2,1)} reshape(bf16[104,128,416]{2,1,0:T(8,128)(2,1)} %copy.95) | data formatting | bytes 22151168 | tf_op jit(solution)/shard_map/convert_element_type | solution.py:16
  415.7 87.5 %reduce = bf16[13312,416]{1,0:T(8,128)(2,1)} reduce(bf16[13312,1,416]{2,1,0:T(2,128)(2,1)} %reshape.155, bf16[]{:T(256)} %broadcast.21), dimensions={1}, to_apply=%reshape.155.reduce_sub_computation | reduce | bytes 22151170 | tf_op jit(solution)/shard_map/convert_element_type | solution.py:16
  659.6 77.6 %reshape.156 = bf16[13312,1,416]{2,1,0:T(2,128)(2,1)} reshape(bf16[104,128,416]{2,1,0:T(8,128)(2,1)} %copy.96) | data formatting | bytes 22151168 | tf_op jit(solution)/shard_map/convert_element_type | solution.py:16
  737.1 87.6 %reduce.1 = bf16[13312,416]{1,0:T(8,128)(2,1)} reduce(bf16[13312,1,416]{2,1,0:T(2,128)(2,1)} %reshape.156, bf16[]{:T(256)} %broadcast.21), dimensions={1}, to_apply=%reshape.156.reduce_sub_computation | reduce | bytes 22151170 | tf_op jit(solution)/shard_map/convert_element_type | solution.py:16
  854.8 30.4 %reshape.160 = bf16[13312,1,416]{2,1,0:T(2,128)(2,1)} reshape(bf16[8,2,346112]{2,1,0:T(2,128)(2,1)} %all-to-all-done.1) | data formatting | bytes 22151168
  885.3 52.5 %copy.68 = bf16[13312,1,416]{0,2,1:T(8,128)(2,1)} copy(bf16[13312,1,416]{2,1,0:T(2,128)(2,1)} %reshape.160) | data formatting | bytes 22151168 | tf_op jit(solution)/shard_map/all_to_all | solution.py:46
  995.2 96.4 %all-to-all-done.3 = bf16[4,2,692224]{2,1,0:T(2,128)(2,1)} async-done(((bf16[4,2,692224]{2,1,0:T(2,128)(2,1)}), bf16[4,2,692224]{2,1,0:T(2,128)(2,1)}, u32[]{:S(2)}, u32[]{:S(2)}) %all-to-all-start.3) | async-done | bytes 11075616 | tf_op jit(solution)/shard_map/all_to_all | solution.py:52
  1091.6 45.3 %reshape.162 = bf16[13312,1,416]{2,1,0:T(2,128)(2,1)} reshape(bf16[4,2,692224]{2,1,0:T(2,128)(2,1)} %all-to-all-done.3) | data formatting | bytes 22151168
  1136.9 52.8 %copy.74 = bf16[13312,1,416]{0,2,1:T(8,128)(2,1)} copy(bf16[13312,1,416]{2,1,0:T(2,128)(2,1)} %reshape.162) | data formatting | bytes 22151168 | tf_op jit(solution)/shard_map/all_to_all | solution.py:52
  1230.7 32.3 %multiply_reduce_fusion.3 = (f32[]{:T(128)}, f32[]{:T(128)}, f32[1664,3328]{1,0:T(8,128)}, f32[1664,3328]{1,0:T(8,128)}) fusion(f32[]{:T(128)S(6)} %max.13, bf16[1664,3328]{1,0:T(8,128)(2,1)} %param.5, f32[1664,3328]{1,0:T(8,128)} %copy.76, f32[3328,4,1,416]{0,3,1,2:T(8,128)} %copy.75, s32[16,13312]{1,0:T(8,128)} %param.9, s32[]{:T(128)S(6)} %select_n.14, ...), kind=kOutput, calls=%fused_computation.21 | convolution fusion | flops 232667136 | bytes 99999760 | tf_op jit(solution)/shard_map/sa,sb->ab/dot_general | solution.py:29
  1263.1 43.3 %all-reduce.1 = (f32[]{:T(128)}, f32[]{:T(128)}) all-reduce(f32[]{:T(128)} %get-tuple-element.6, f32[]{:T(128)} %get-tuple-element.5), channel_id=1, replica_groups=mesh['up'=8,'dn'=4] {'up','dn'}, use_global_device_ids=true, to_apply=%region_5.0 | all-reduce | flops 2 | bytes 16 | tf_op jit(solution)/shard_map/psum | solution.py:60
  1348.6 127.0 %all_to_all.97 = bf16[1664,8,416]{0,2,1:T(8,128)(2,1)} all-to-all(bf16[1664,8,416]{0,2,1:T(8,128)(2,1)} %bitcast.113), channel_id=1, replica_groups=mesh['up'=8,'dn'=4] {'up'}, dimensions={1} | all-to-all | bytes 22151168 | tf_op jit(solution)/shard_map/all_to_all | solution.py:43
  1604.5 77.7 %reshape.157 = bf16[13312,1,416]{2,1,0:T(2,128)(2,1)} reshape(bf16[104,128,416]{2,1,0:T(8,128)(2,1)} %copy.97) | data formatting | bytes 22151168 | tf_op jit(solution)/shard_map/convert_element_type | solution.py:16
  1682.3 87.5 %reduce.2 = bf16[13312,416]{1,0:T(8,128)(2,1)} reduce(bf16[13312,1,416]{2,1,0:T(2,128)(2,1)} %reshape.157, bf16[]{:T(256)} %broadcast.21), dimensions={1}, to_apply=%reshape.157.reduce_sub_computation | reduce | bytes 22151170 | tf_op jit(solution)/shard_map/convert_element_type | solution.py:16
  1926.1 77.6 %reshape.158 = bf16[13312,1,416]{2,1,0:T(2,128)(2,1)} reshape(bf16[104,128,416]{2,1,0:T(8,128)(2,1)} %copy.98) | data formatting | bytes 22151168 | tf_op jit(solution)/shard_map/convert_element_type | solution.py:16
  2003.7 87.6 %reduce.3 = bf16[13312,416]{1,0:T(8,128)(2,1)} reduce(bf16[13312,1,416]{2,1,0:T(2,128)(2,1)} %reshape.158, bf16[]{:T(256)} %broadcast.21), dimensions={1}, to_apply=%reshape.158.reduce_sub_computation | reduce | bytes 22151170 | tf_op jit(solution)/shard_map/convert_element_type | solution.py:16
  2150.5 52.5 %copy.82 = bf16[13312,1,416]{0,2,1:T(8,128)(2,1)} copy(bf16[13312,1,416]{2,1,0:T(2,128)(2,1)} %reshape.164) | data formatting | bytes 22151168 | tf_op jit(solution)/shard_map/all_to_all | solution.py:46
  2260.5 97.7 %all-to-all-done.7 = bf16[4,2,692224]{2,1,0:T(2,128)(2,1)} async-done(((bf16[4,2,692224]{2,1,0:T(2,128)(2,1)}), bf16[4,2,692224]{2,1,0:T(2,128)(2,1)}, u32[]{:S(2)}, u32[]{:S(2)}) %all-to-all-start.7) | async-done | bytes 11075616 | tf_op jit(solution)/shard_map/all_to_all | solution.py:52
  2358.2 45.3 %reshape.166 = bf16[13312,1,416]{2,1,0:T(2,128)(2,1)} reshape(bf16[4,2,692224]{2,1,0:T(2,128)(2,1)} %all-to-all-done.7) | data formatting | bytes 22151168
  2403.5 52.7 %copy.88 = bf16[13312,1,416]{0,2,1:T(8,128)(2,1)} copy(bf16[13312,1,416]{2,1,0:T(2,128)(2,1)} %reshape.166) | data formatting | bytes 22151168 | tf_op jit(solution)/shard_map/all_to_all | solution.py:52
  2497.1 40.2 %multiply_reduce_fusion.1 = (f32[]{:T(128)}, f32[]{:T(128)}, f32[1664,3328]{1,0:T(8,128)}) fusion(f32[1664,3328]{1,0:T(8,128)} %get-tuple-element.13, f32[]{:T(128)S(6)} %max.13, bf16[1664,3328]{1,0:T(8,128)(2,1)} %param.5, f32[]{:T(128)} %sqrt.10, f32[1664,3328]{1,0:T(8,128)} %get-tuple-element.15, f32[1664,3328]{1,0:T(8,128)} %copy.90, ...), kind=kLoop, calls=%fused_computation.18 | loop fusion | flops 66453504 | bytes 121831440 | tf_op jit(solution)/shard_map/reduce_sum | solution.py:60
  2537.3 42.5 %all-reduce = (f32[]{:T(128)}, f32[]{:T(128)}) all-reduce(f32[]{:T(128)} %get-tuple-element.4, f32[]{:T(128)} %get-tuple-element.3), channel_id=1, replica_groups=mesh['up'=8,'dn'=4] {'up','dn'}, use_global_device_ids=true, to_apply=%region_9.0 | all-reduce | flops 2 | bytes 16 | tf_op jit(solution)/shard_map/psum | solution.py:60
  (77 shorter events, 954.8 us)
Async XLA Ops:
  80.3 133.9 %copy-start.4 = (s32[104,5]{0,1:T(8,128)S(1)}, s32[104,5]{0,1:T(8,128)}, u32[]{:S(2)}) copy-start(s32[104,5]{0,1:T(8,128)} %param.8) | copy-start | bytes 6244
  80.3 134.0 %copy-start.5 = (s32[104,5]{0,1:T(8,128)S(1)}, s32[104,5]{0,1:T(8,128)}, u32[]{:S(2)}) copy-start(s32[104,5]{0,1:T(8,128)} %param.7) | copy-start | bytes 6244
  207.5 317.4 %all-to-all-start.2 = ((bf16[3328,4,416]{0,2,1:T(8,128)(2,1)}), bf16[3328,4,416]{0,2,1:T(8,128)(2,1)}, u32[]{:S(2)}, u32[]{:S(2)}) async-start(bf16[3328,4,416]{0,2,1:T(8,128)(2,1)} %bitcast.96), calls=%async_computation.2 | async-start | bytes 22151168 | tf_op jit(solution)/shard_map/all_to_all | solution.py:49
  214.3 399.5 %copy-start.2 = (bf16[104,5]{1,0:T(8,128)(2,1)}, bf16[104,5]{1,0:T(8,128)(2,1)S(1)}, u32[]{:S(2)}) copy-start(bf16[104,5]{1,0:T(8,128)(2,1)S(1)} %copy.61) | copy-start | bytes 3124
  214.7 372.7 %copy-start = (s32[1024]{0:T(1024)}, s32[1024]{0:T(1024)S(1)}, u32[]{:S(2)}) copy-start(s32[1024]{0:T(1024)S(1)} %pad_clamp_fusion) | copy-start | bytes 12292
  524.9 322.3 %all-to-all-start.1 = ((bf16[8,2,346112]{2,1,0:T(2,128)(2,1)}), bf16[8,2,346112]{2,1,0:T(2,128)(2,1)}, u32[]{:S(2)}, u32[]{:S(2)}) async-start(bf16[8,2,346112]{2,1,0:T(2,128)(2,1)} %reshape.159), calls=%async_computation.1 | async-start | bytes 22151168 | tf_op jit(solution)/shard_map/all_to_all | solution.py:46
  847.2 244.5 %all-to-all-start.3 = ((bf16[4,2,692224]{2,1,0:T(2,128)(2,1)}), bf16[4,2,692224]{2,1,0:T(2,128)(2,1)}, u32[]{:S(2)}, u32[]{:S(2)}) async-start(bf16[4,2,692224]{2,1,0:T(2,128)(2,1)} %reshape.161), calls=%async_computation.3 | async-start | bytes 22151168 | tf_op jit(solution)/shard_map/all_to_all | solution.py:52
  1475.6 315.9 %all-to-all-start.6 = ((bf16[3328,4,416]{0,2,1:T(8,128)(2,1)}), bf16[3328,4,416]{0,2,1:T(8,128)(2,1)}, u32[]{:S(2)}, u32[]{:S(2)}) async-start(bf16[3328,4,416]{0,2,1:T(8,128)(2,1)} %bitcast.97), calls=%async_computation.6 | async-start | bytes 22151168 | tf_op jit(solution)/shard_map/all_to_all | solution.py:49
  1500.6 31.8 %copy-start.1 = (s32[1024]{0:T(1024)S(1)}, s32[1024]{0:T(1024)}, u32[]{:S(2)}) copy-start(s32[1024]{0:T(1024)} %copy-done) | copy-start | bytes 12292
  1532.3 26.5 %copy-start.3 = (bf16[104,5]{1,0:T(8,128)(2,1)S(1)}, bf16[104,5]{1,0:T(8,128)(2,1)}, u32[]{:S(2)}) copy-start(bf16[104,5]{1,0:T(8,128)(2,1)} %copy-done.2) | copy-start | bytes 3124
  1791.5 322.3 %all-to-all-start.5 = ((bf16[8,2,346112]{2,1,0:T(2,128)(2,1)}), bf16[8,2,346112]{2,1,0:T(2,128)(2,1)}, u32[]{:S(2)}, u32[]{:S(2)}) async-start(bf16[8,2,346112]{2,1,0:T(2,128)(2,1)} %reshape.163), calls=%async_computation.5 | async-start | bytes 22151168 | tf_op jit(solution)/shard_map/all_to_all | solution.py:46
  2113.7 244.5 %all-to-all-start.7 = ((bf16[4,2,692224]{2,1,0:T(2,128)(2,1)}), bf16[4,2,692224]{2,1,0:T(2,128)(2,1)}, u32[]{:S(2)}, u32[]{:S(2)}) async-start(bf16[4,2,692224]{2,1,0:T(2,128)(2,1)} %reshape.165), calls=%async_computation.7 | async-start | bytes 22151168 | tf_op jit(solution)/shard_map/all_to_all | solution.py:52
where the time goes:
time: 2630 us; the launch traced here: 2600 us
  local copies, waits for them, and re-layouts  1360 us (52%)
  other arithmetic  469 us (18%)
  blocking collectives  381 us (14%)
  waiting for transfers between devices  194 us (7%)
  matrix products  150 us (6%)
  starting transfers between devices  39.6 us (2%)
    convert_element_type x9, local copies, waits for them, and re-layouts, hop_lead(): return result.reshape(layout).astype(jnp.bfloat16)  376 us
    convert_element_type x4, other arithmetic, hop_lead(): return result.reshape(layout).astype(jnp.bfloat16)  350 us
    unnamed x22, local copies, waits for them, and re-layouts  257 us
    all_to_all x2, blocking collectives, body(): lax.all_to_all(cube, 'up', split_axis=1, concat_axis=0, tiled=True)  254 us
    all_to_all x2, waiting for transfers between devices, body(): lax.all_to_all(hopped, 'dn', split_axis=0, concat_axis=1, tiled=True)  194 us
    another operation x8, local copies, waits for them, and re-layouts, hop_lead(): cube = matrix.reshape(layout[0] // tile_width, tile_width, -1)  122 us
    dot_general x4, matrix products, hop_lead(): jnp.einsum('ikab,ikbm->iam', signed, picked, preferred_element_type=jnp.f...  118 us
    gather x4, local copies, waits for them, and re-layouts, hop_lead(): picked = cube[tile_columns]  106 us
  transfers between devices with their start and end apart: 6, of which 2 were waited for; matrix products, arithmetic and copies ran while one was open for 59% of the time, Pallas kernels for 0%

commit v1 on v0

--- a/solution.py
+++ b/solution.py
@@ -49,7 +49,15 @@
         part = lax.all_to_all(flipped, "dn", split_axis=1, concat_axis=0, tiled=True)
         whole = part.reshape(part.shape[0], part.shape[2])
         hopped = hop_lead(whole, signed, tile_columns).reshape(part.shape)
-        returned = lax.all_to_all(hopped, "dn", split_axis=0, concat_axis=1, tiled=True)
+        ways, here = (lax.axis_size("dn"), lax.axis_index("dn"))
+        width = hopped.shape[0] // ways
+        turned = jnp.roll(hopped, -here * width, axis=0)
+        got = [lax.slice_in_dim(turned, 0, width, axis=0)]
+        for far in range(1, ways):
+            sent = lax.slice_in_dim(turned, far * width, (far + 1) * width, axis=0)
+            got.append(lax.ppermute(sent, "dn", [(d, (d + far) % ways) for d in range(ways)]))
+        line = jnp.concatenate(got[::-1], axis=1)
+        returned = jnp.roll(line, (here + 1) * got[0].shape[1], axis=1)
         hopped_down = returned.reshape(block_cols, block_rows).T
         work = (
             hopped_up.astype(jnp.float32)

time: 2630 us -> 2200 us (0.84)
  local copies, waits for them, and re-layouts: 1360 us -> 928 us
  waiting for transfers between devices: 194 us -> 329 us
  other arithmetic: 469 us -> 346 us
    ppermute x0 -> x6, waiting for transfers between devices: none -> 329 us  [body(): lax.ppermute(sent, 'dn', [(d, (d + far) % ways) for d in range(ways)])]
    all_to_all x2 -> x0, waiting for transfers between devices: 194 us -> none  [body(): lax.all_to_all(hopped, 'dn', split_axis=0, concat_axis=1, tiled=True)]
    convert_element_type x4 -> x2, other arithmetic: 350 us -> 175 us  [hop_lead(): return result.reshape(layout).astype(jnp.bfloat16)]
    unnamed x22 -> x18, local copies, waits for them, and re-layouts: 257 us -> 122 us
    convert_element_type x9, local copies, waits for them, and re-layouts: 376 us -> 260 us  [hop_lead(): return result.reshape(layout).astype(jnp.bfloat16)]
    all_to_all x2 -> x0, local copies, waits for them, and re-layouts: 106 us -> none  [body(): lax.all_to_all(hopped, 'dn', split_axis=0, concat_axis=1, tiled=True)]
    convert_element_type x4 -> x0, local copies, waits for them, and re-layouts: 81.9 us -> none  [body(): hopped_down.astype(jnp.float32)]
    concatenate x0 -> x4, other arithmetic: none -> 54.9 us  [the longest x2 33.2 us: body(): returned = jnp.roll(line, (here + 1) * got[0].shape[1], axis=1)]
  transfers between devices with their start and end apart: 6 -> 10, of which waited for: 2 -> 5; matrix products, arithmetic and copies ran while one was open for 59% -> 50% of each run, Pallas kernels for 0% -> 0%
where the time goes in v1:
time: 2200 us; the launch traced here: 2180 us
  local copies, waits for them, and re-layouts  928 us (42%)
  blocking collectives  378 us (17%)
  other arithmetic  346 us (16%)
  waiting for transfers between devices  329 us (15%)
  matrix products  148 us (7%)
  starting transfers between devices  39.4 us (2%)
    ppermute x6, waiting for transfers between devices, body(): lax.ppermute(sent, 'dn', [(d, (d + far) % ways) for d in range(ways)])  329 us
    convert_element_type x9, local copies, waits for them, and re-layouts, hop_lead(): return result.reshape(layout).astype(jnp.bfloat16)  260 us
    all_to_all x2, blocking collectives, body(): lax.all_to_all(cube, 'up', split_axis=1, concat_axis=0, tiled=True)  254 us
    convert_element_type x2, other arithmetic, hop_lead(): return result.reshape(layout).astype(jnp.bfloat16)  175 us
    another operation x8, local copies, waits for them, and re-layouts, hop_lead(): cube = matrix.reshape(layout[0] // tile_width, tile_width, -1)  122 us
    unnamed x18, local copies, waits for them, and re-layouts  122 us
    dot_general x4, matrix products, hop_lead(): jnp.einsum('ikab,ikbm->iam', signed, picked, preferred_element_type=jnp.f...  118 us
    gather x4, local copies, waits for them, and re-layouts, hop_lead(): picked = cube[tile_columns]  106 us
  transfers between devices with their start and end apart: 10, of which 5 were waited for; matrix products, arithmetic and copies ran while one was open for 50% of the time, Pallas kernels for 0%

profile of v1, /device:TPU:12, one launch (start us, length us, event | category | flops | bytes accessed | tf_op | source)
XLA Modules:
  0.0 2177.8 jit_solution(12280559423834406255)
XLA Ops:
  11.1 41.6 %psum.35 = f32[]{:T(128)} all-reduce(f32[]{:T(128)} %fusion), channel_id=1, replica_groups=mesh['up'=8,'dn'=4] {'up','dn'}, use_global_device_ids=true, to_apply=%region_1.0 | all-reduce | flops 1 | bytes 8 | tf_op jit(solution)/shard_map/psum | solution.py:33
  80.3 127.1 %all_to_all.78 = bf16[1664,8,416]{0,2,1:T(8,128)(2,1)} all-to-all(bf16[1664,8,416]{0,2,1:T(8,128)(2,1)} %bitcast.116), channel_id=1, replica_groups=mesh['up'=8,'dn'=4] {'up'}, dimensions={1} | all-to-all | bytes 22151168 | tf_op jit(solution)/shard_map/all_to_all | solution.py:43
  291.6 29.5 %bitcast_convert_fusion.3 = bf16[104,128,416]{1,2,0:T(8,128)(2,1)} fusion(bf16[104,5,128,416]{2,3,1,0:T(8,128)(2,1)} %bitcast.111, bf16[104,5,128,128]{3,2,1,0:T(8,128)(2,1)} %param.10, bf16[104,5]{1,0:T(8,128)(2,1)S(1)} %copy.53), kind=kOutput, calls=%fused_computation.37 | convolution fusion | flops 7102431232 | bytes 83493904 | tf_op jit(solution)/shard_map/ikab,ikbm->iam/dot_general | solution.py:15
  337.4 77.8 %reshape.147 = bf16[13312,1,416]{2,1,0:T(2,128)(2,1)} reshape(bf16[104,128,416]{2,1,0:T(8,128)(2,1)} %copy.81) | data formatting | bytes 22151168 | tf_op jit(solution)/shard_map/convert_element_type | solution.py:16
  415.7 87.5 %reduce = bf16[13312,416]{1,0:T(8,128)(2,1)} reduce(bf16[13312,1,416]{2,1,0:T(2,128)(2,1)} %reshape.147, bf16[]{:T(256)} %broadcast.22), dimensions={1}, to_apply=%reshape.147.reduce_sub_computation | reduce | bytes 22151170 | tf_op jit(solution)/shard_map/convert_element_type | solution.py:16
  614.0 29.4 %bitcast_convert_fusion.2 = bf16[104,128,416]{1,2,0:T(8,128)(2,1)} fusion(bf16[104,5,128,416]{2,3,1,0:T(8,128)(2,1)} %bitcast.112, bf16[104,5,128,128]{3,2,1,0:T(8,128)(2,1)} %param.10, bf16[104,5]{1,0:T(8,128)(2,1)S(1)} %copy.53), kind=kOutput, calls=%fused_computation.36 | convolution fusion | flops 7102431232 | bytes 83493904 | tf_op jit(solution)/shard_map/ikab,ikbm->iam/dot_general | solution.py:15
  699.7 30.6 %reshape.150 = bf16[13312,1,416]{2,1,0:T(2,128)(2,1)} reshape(bf16[8,2,346112]{2,1,0:T(2,128)(2,1)} %all-to-all-done.1) | data formatting | bytes 22151168
  730.3 52.5 %copy.60 = bf16[13312,1,416]{0,2,1:T(8,128)(2,1)} copy(bf16[13312,1,416]{2,1,0:T(2,128)(2,1)} %reshape.150) | data formatting | bytes 22151168 | tf_op jit(solution)/shard_map/all_to_all | solution.py:46
  840.2 34.8 %collective-permute-done.1 = bf16[3328,1,416]{0,2,1:T(8,128)(2,1)} collective-permute-done((bf16[3328,1,416]{0,2,1:T(8,128)(2,1)}, bf16[3328,1,416]{0,2,1:T(8,128)(2,1)}, u32[]{:S(2)}, u32[]{:S(2)}) %collective-permute-start.1) | collective-permute-done | bytes 2768928 | tf_op jit(solution)/shard_map/ppermute | solution.py:58
  875.0 58.7 %collective-permute-done.2 = bf16[3328,1,416]{0,2,1:T(8,128)(2,1)} collective-permute-done((bf16[3328,1,416]{0,2,1:T(8,128)(2,1)}, bf16[3328,1,416]{0,2,1:T(8,128)(2,1)}, u32[]{:S(2)}, u32[]{:S(2)}) %collective-permute-start.2) | collective-permute-done | bytes 2768928 | tf_op jit(solution)/shard_map/ppermute | solution.py:58
  950.2 29.9 %multiply_reduce_fusion.3 = (f32[]{:T(128)}, f32[]{:T(128)}, f32[1664,3328]{1,0:T(8,128)}, f32[1664,3328]{1,0:T(8,128)}) fusion(f32[]{:T(128)S(6)} %max.13, bf16[1664,3328]{1,0:T(8,128)(2,1)} %param.9, f32[1664,3328]{1,0:T(8,128)} %copy.65, bf16[3328,4,416]{0,2,1:T(8,128)(2,1)} %fusion.17, s32[16,13312]{1,0:T(8,128)} %param.13, s32[]{:T(128)S(6)} %select_n.31, ...), kind=kOutput, calls=%fused_computation.43 | convolution fusion | flops 238204928 | bytes 88924176 | tf_op jit(solution)/shard_map/sa,sb->ab/dot_general | solution.py:29
  980.0 41.1 %all-reduce.1 = (f32[]{:T(128)}, f32[]{:T(128)}) all-reduce(f32[]{:T(128)} %get-tuple-element.8, f32[]{:T(128)} %get-tuple-element.7), channel_id=1, replica_groups=mesh['up'=8,'dn'=4] {'up','dn'}, use_global_device_ids=true, to_apply=%region_5.8 | all-reduce | flops 2 | bytes 16 | tf_op jit(solution)/shard_map/psum | solution.py:68
  1063.4 127.0 %all_to_all.79 = bf16[1664,8,416]{0,2,1:T(8,128)(2,1)} all-to-all(bf16[1664,8,416]{0,2,1:T(8,128)(2,1)} %bitcast.117), channel_id=1, replica_groups=mesh['up'=8,'dn'=4] {'up'}, dimensions={1} | all-to-all | bytes 22151168 | tf_op jit(solution)/shard_map/all_to_all | solution.py:43
  1275.7 29.4 %bitcast_convert_fusion.1 = bf16[104,128,416]{1,2,0:T(8,128)(2,1)} fusion(bf16[104,5,128,416]{2,3,1,0:T(8,128)(2,1)} %bitcast.113, bf16[104,5,128,128]{3,2,1,0:T(8,128)(2,1)} %param.10, bf16[104,5]{1,0:T(8,128)(2,1)S(1)} %copy-done.3), kind=kOutput, calls=%fused_computation.35 | convolution fusion | flops 7102431232 | bytes 83493904 | tf_op jit(solution)/shard_map/ikab,ikbm->iam/dot_general | solution.py:15
  1321.4 77.7 %reshape.148 = bf16[13312,1,416]{2,1,0:T(2,128)(2,1)} reshape(bf16[104,128,416]{2,1,0:T(8,128)(2,1)} %copy.82) | data formatting | bytes 22151168 | tf_op jit(solution)/shard_map/convert_element_type | solution.py:16
  1399.1 87.5 %reduce.1 = bf16[13312,416]{1,0:T(8,128)(2,1)} reduce(bf16[13312,1,416]{2,1,0:T(2,128)(2,1)} %reshape.148, bf16[]{:T(256)} %broadcast.22), dimensions={1}, to_apply=%reshape.148.reduce_sub_computation | reduce | bytes 22151170 | tf_op jit(solution)/shard_map/convert_element_type | solution.py:16
  1597.0 29.4 %bitcast_convert_fusion = bf16[104,128,416]{1,2,0:T(8,128)(2,1)} fusion(bf16[104,5,128,416]{2,3,1,0:T(8,128)(2,1)} %bitcast.110, bf16[104,5,128,128]{3,2,1,0:T(8,128)(2,1)} %param.10, bf16[104,5]{1,0:T(8,128)(2,1)S(1)} %copy-done.3), kind=kOutput, calls=%fused_computation.34 | convolution fusion | flops 7102431232 | bytes 83493904 | tf_op jit(solution)/shard_map/ikab,ikbm->iam/dot_general | solution.py:15
  1681.6 58.7 %collective-permute-done.3 = bf16[3328,1,416]{0,2,1:T(8,128)(2,1)} collective-permute-done((bf16[3328,1,416]{0,2,1:T(8,128)(2,1)}, bf16[3328,1,416]{0,2,1:T(8,128)(2,1)}, u32[]{:S(2)}, u32[]{:S(2)}) %collective-permute-start.3) | collective-permute-done | bytes 2768928 | tf_op jit(solution)/shard_map/ppermute | solution.py:58
  1740.3 117.9 %collective-permute-done.4 = bf16[3328,1,416]{0,2,1:T(8,128)(2,1)} collective-permute-done((bf16[3328,1,416]{0,2,1:T(8,128)(2,1)}, bf16[3328,1,416]{0,2,1:T(8,128)(2,1)}, u32[]{:S(2)}, u32[]{:S(2)}) %collective-permute-start.4) | collective-permute-done | bytes 2768928 | tf_op jit(solution)/shard_map/ppermute | solution.py:58
  1858.2 58.7 %collective-permute-done.5 = bf16[3328,1,416]{0,2,1:T(8,128)(2,1)} collective-permute-done((bf16[3328,1,416]{0,2,1:T(8,128)(2,1)}, bf16[3328,1,416]{0,2,1:T(8,128)(2,1)}, u32[]{:S(2)}, u32[]{:S(2)}) %collective-permute-start.5) | collective-permute-done | bytes 2768928 | tf_op jit(solution)/shard_map/ppermute | solution.py:58
  1933.7 30.4 %reshape.152 = bf16[13312,1,416]{2,1,0:T(2,128)(2,1)} reshape(bf16[8,2,346112]{2,1,0:T(2,128)(2,1)} %all-to-all-done.4) | data formatting | bytes 22151168
  1964.1 52.5 %copy.71 = bf16[13312,1,416]{0,2,1:T(8,128)(2,1)} copy(bf16[13312,1,416]{2,1,0:T(2,128)(2,1)} %reshape.152) | data formatting | bytes 22151168 | tf_op jit(solution)/shard_map/all_to_all | solution.py:46
  2074.0 37.2 %multiply_reduce_fusion.1 = (f32[]{:T(128)}, f32[]{:T(128)}, f32[1664,3328]{1,0:T(8,128)}) fusion(f32[1664,3328]{1,0:T(8,128)} %get-tuple-element.15, f32[]{:T(128)S(6)} %max.13, bf16[1664,3328]{1,0:T(8,128)(2,1)} %param.9, f32[]{:T(128)} %sqrt.10, f32[1664,3328]{1,0:T(8,128)} %get-tuple-element.25, f32[1664,3328]{1,0:T(8,128)} %copy.76, ...), kind=kLoop, calls=%fused_computation.40 | loop fusion | flops 71991296 | bytes 110755856 | tf_op jit(solution)/shard_map/reduce_sum | solution.py:68
  2111.2 41.2 %all-reduce = (f32[]{:T(128)}, f32[]{:T(128)}) all-reduce(f32[]{:T(128)} %get-tuple-element.6, f32[]{:T(128)} %get-tuple-element.5), channel_id=1, replica_groups=mesh['up'=8,'dn'=4] {'up','dn'}, use_global_device_ids=true, to_apply=%region_9.12 | all-reduce | flops 2 | bytes 16 | tf_op jit(solution)/shard_map/psum | solution.py:68
  (79 shorter events, 779.8 us)
Async XLA Ops:
  80.3 133.9 %copy-start.5 = (s32[104,5]{0,1:T(8,128)S(1)}, s32[104,5]{0,1:T(8,128)}, u32[]{:S(2)}) copy-start(s32[104,5]{0,1:T(8,128)} %param.11) | copy-start | bytes 6244
  80.3 134.2 %copy-start.4 = (s32[104,5]{0,1:T(8,128)S(1)}, s32[104,5]{0,1:T(8,128)}, u32[]{:S(2)}) copy-start(s32[104,5]{0,1:T(8,128)} %param.12) | copy-start | bytes 6244
  207.5 317.5 %all-to-all-start.2 = ((bf16[3328,4,416]{0,2,1:T(8,128)(2,1)}), bf16[3328,4,416]{0,2,1:T(8,128)(2,1)}, u32[]{:S(2)}, u32[]{:S(2)}) async-start(bf16[3328,4,416]{0,2,1:T(8,128)(2,1)} %bitcast.102), calls=%async_computation.2 | async-start | bytes 22151168 | tf_op jit(solution)/shard_map/all_to_all | solution.py:49
  214.7 399.3 %copy-start.2 = (bf16[104,5]{1,0:T(8,128)(2,1)}, bf16[104,5]{1,0:T(8,128)(2,1)S(1)}, u32[]{:S(2)}) copy-start(bf16[104,5]{1,0:T(8,128)(2,1)S(1)} %copy.53) | copy-start | bytes 3124
  214.7 372.8 %copy-start = (s32[1024]{0:T(1024)}, s32[1024]{0:T(1024)S(1)}, u32[]{:S(2)}) copy-start(s32[1024]{0:T(1024)S(1)} %pad_clamp_fusion) | copy-start | bytes 12292
  524.9 174.7 %all-to-all-start.1 = ((bf16[8,2,346112]{2,1,0:T(2,128)(2,1)}), bf16[8,2,346112]{2,1,0:T(2,128)(2,1)}, u32[]{:S(2)}, u32[]{:S(2)}) async-start(bf16[8,2,346112]{2,1,0:T(2,128)(2,1)} %reshape.149), calls=%async_computation.1 | async-start | bytes 22151168 | tf_op jit(solution)/shard_map/all_to_all | solution.py:46
  693.1 147.1 %collective-permute-start = (bf16[3328,1,416]{0,2,1:T(8,128)(2,1)}, bf16[3328,1,416]{0,2,1:T(8,128)(2,1)}, u32[]{:S(2)}, u32[]{:S(2)}) collective-permute-start(bf16[3328,1,416]{0,2,1:T(8,128)(2,1)} %get-tuple-element.24), channel_id=1, source_target_pairs={{0,3},{1,0},{2,1},{3,2},{4,7},{5,4},{6,5},{7,6},{8,11},{9,8},{10,9... | collective-permute-start | bytes 8306696 | tf_op jit(solution)/shard_map/ppermute | solution.py:58
  693.2 181.9 %collective-permute-start.1 = (bf16[3328,1,416]{0,2,1:T(8,128)(2,1)}, bf16[3328,1,416]{0,2,1:T(8,128)(2,1)}, u32[]{:S(2)}, u32[]{:S(2)}) collective-permute-start(bf16[3328,1,416]{0,2,1:T(8,128)(2,1)} %get-tuple-element.23), channel_id=1, source_target_pairs={{0,2},{1,3},{2,0},{3,1},{4,6},{5,7},{6,4},{7,5},{8,10},{9,11},{10,... | collective-permute-start | bytes 8306696 | tf_op jit(solution)/shard_map/ppermute | solution.py:58
  696.1 237.7 %collective-permute-start.2 = (bf16[3328,1,416]{0,2,1:T(8,128)(2,1)}, bf16[3328,1,416]{0,2,1:T(8,128)(2,1)}, u32[]{:S(2)}, u32[]{:S(2)}) collective-permute-start(bf16[3328,1,416]{0,2,1:T(8,128)(2,1)} %get-tuple-element.22), channel_id=1, source_target_pairs={{0,1},{1,2},{2,3},{3,0},{4,5},{5,6},{6,7},{7,4},{8,9},{9,10},{10,1... | collective-permute-start | bytes 8306696 | tf_op jit(solution)/shard_map/ppermute | solution.py:58
  1190.4 317.9 %all-to-all-start.5 = ((bf16[3328,4,416]{0,2,1:T(8,128)(2,1)}), bf16[3328,4,416]{0,2,1:T(8,128)(2,1)}, u32[]{:S(2)}, u32[]{:S(2)}) async-start(bf16[3328,4,416]{0,2,1:T(8,128)(2,1)} %bitcast.103), calls=%async_computation.5 | async-start | bytes 22151168 | tf_op jit(solution)/shard_map/all_to_all | solution.py:49
  1217.4 31.8 %copy-start.1 = (s32[1024]{0:T(1024)S(1)}, s32[1024]{0:T(1024)}, u32[]{:S(2)}) copy-start(s32[1024]{0:T(1024)} %copy-done) | copy-start | bytes 12292
  1249.2 26.5 %copy-start.3 = (bf16[104,5]{1,0:T(8,128)(2,1)S(1)}, bf16[104,5]{1,0:T(8,128)(2,1)}, u32[]{:S(2)}) copy-start(bf16[104,5]{1,0:T(8,128)(2,1)} %copy-done.2) | copy-start | bytes 3124
  1508.3 425.4 %all-to-all-start.4 = ((bf16[8,2,346112]{2,1,0:T(2,128)(2,1)}), bf16[8,2,346112]{2,1,0:T(2,128)(2,1)}, u32[]{:S(2)}, u32[]{:S(2)}) async-start(bf16[8,2,346112]{2,1,0:T(2,128)(2,1)} %reshape.151), calls=%async_computation.4 | async-start | bytes 22151168 | tf_op jit(solution)/shard_map/all_to_all | solution.py:46
  1676.3 64.0 %collective-permute-start.3 = (bf16[3328,1,416]{0,2,1:T(8,128)(2,1)}, bf16[3328,1,416]{0,2,1:T(8,128)(2,1)}, u32[]{:S(2)}, u32[]{:S(2)}) collective-permute-start(bf16[3328,1,416]{0,2,1:T(8,128)(2,1)} %get-tuple-element.20), channel_id=1, source_target_pairs={{0,3},{1,0},{2,1},{3,2},{4,7},{5,4},{6,5},{7,6},{8,11},{9,8},{10,9... | collective-permute-start | bytes 8306696 | tf_op jit(solution)/shard_map/ppermute | solution.py:58
  1676.3 181.9 %collective-permute-start.4 = (bf16[3328,1,416]{0,2,1:T(8,128)(2,1)}, bf16[3328,1,416]{0,2,1:T(8,128)(2,1)}, u32[]{:S(2)}, u32[]{:S(2)}) collective-permute-start(bf16[3328,1,416]{0,2,1:T(8,128)(2,1)} %get-tuple-element.19), channel_id=1, source_target_pairs={{0,2},{1,3},{2,0},{3,1},{4,6},{5,7},{6,4},{7,5},{8,10},{9,11},{10,... | collective-permute-start | bytes 8306696 | tf_op jit(solution)/shard_map/ppermute | solution.py:58
  1679.2 237.7 %collective-permute-start.5 = (bf16[3328,1,416]{0,2,1:T(8,128)(2,1)}, bf16[3328,1,416]{0,2,1:T(8,128)(2,1)}, u32[]{:S(2)}, u32[]{:S(2)}) collective-permute-start(bf16[3328,1,416]{0,2,1:T(8,128)(2,1)} %get-tuple-element.18), channel_id=1, source_target_pairs={{0,1},{1,2},{2,3},{3,0},{4,5},{5,6},{6,7},{7,4},{8,9},{9,10},{10,1... | collective-permute-start | bytes 8306696 | tf_op jit(solution)/shard_map/ppermute | solution.py:58
